TPU v7x, 32 devices: a whole 2x2x4 slice. The times are simulated.
32 devices in a mesh: dp: 16 (over z, x, core), mp: 2 (over y).
Axes of the slice: x: 2, y: 2, z: 4, core: 2. Of those that a mesh axis runs over, the one named last changes fastest.
Arguments:
- inputs_store: bfloat16 [512, 128], replicated, may hold values from -6 to 6
- window: int32 [16], replicated, may hold values from 0 to 511
- targets_store: bfloat16 [512, 4096], P(None, ('dp', 'mp')), may hold values from -6 to 6
- jac_store: bfloat16 [512, 4096, 128], P(None, ('dp', 'mp')), may hold values from -4 to 4
- first_weight: bfloat16 [128, 1024], replicated, may hold values from -0.5 to 0.5
- first_bias: bfloat16 [1024], replicated, may hold values from -3 to 3
- hidden_weight: bfloat16 [1024, 1024], P(None, 'mp'), may hold values from -0.1875 to 0.1875
- hidden_bias: bfloat16 [1024], P('mp'), may hold values from -3 to 3
- decoder_weight: bfloat16 [4096, 1024], P(('dp', 'mp')), may hold values from -0.1875 to 0.1875
Outputs:
- first_weights: float32 [128, 1024], replicated
- first_biases: float32 [1024], replicated
- hidden_weights: float32 [1024, 1024], P(None, 'mp')
- hidden_biases: float32 [1024], P('mp')
- decoder_grad: float32 [4096, 1024], P(('dp', 'mp'))
Inputs may be any that keep to these rules, and one draw needn't show every extreme that they name: `window`: indices of stored samples; an index may repeat.
All inputs are finite; a program needn't handle non-finite values.
Results may differ from a plain program's by a relative error of at most 0.011.
Values may be sent and summed in bfloat16 or wider, within the bound.
No kernel may reach another device: no remote copies, remote signals or barrier semaphores. Data moves between devices by JAX's collectives and lax.ppermute only.
A program may use at most 64 MiB of HBM per device.

v0:
```python
import jax
import jax.numpy as jnp
from jax import lax
from jax.sharding import PartitionSpec as P


def on_device(
    inputs_store,
    window,
    targets_store,
    jac_store,
    first_weight,
    first_bias,
    hidden_weight,
    hidden_bias,
    decoder_weight,
):
    each_count = window.shape[0] // lax.axis_size("dp")
    jac_window = jac_store[window]
    target_window = targets_store[window]
    jac_mine, target_mine = (
        lax.all_to_all(jac_window, "dp", split_axis=0, concat_axis=1, tiled=True),
        lax.all_to_all(target_window, "dp", split_axis=0, concat_axis=1, tiled=True),
    )
    mine_index = lax.dynamic_slice_in_dim(window, lax.axis_index("dp") * each_count, each_count)
    inputs = inputs_store[mine_index]
    weight_one = first_weight.astype(jnp.float32)
    first_pre = jnp.dot(
        inputs, first_weight, preferred_element_type=jnp.float32
    ) + first_bias.astype(jnp.float32)
    first_act = jnp.tanh(first_pre)
    first_slope = 1.0 - first_act * first_act
    first_tan = (first_slope[:, None, :] * weight_one[None]).astype(jnp.bfloat16)
    first_round = first_act.astype(jnp.bfloat16)
    hidden_lin = jnp.einsum(
        "srh,hk->srk", first_tan, hidden_weight, preferred_element_type=jnp.float32
    )
    hidden_pre = jnp.dot(
        first_round, hidden_weight, preferred_element_type=jnp.float32
    ) + hidden_bias.astype(jnp.float32)
    hidden_act = jnp.tanh(hidden_pre)
    hidden_slope = 1.0 - hidden_act * hidden_act
    hidden_tangent = (hidden_slope[:, None, :] * hidden_lin).astype(jnp.bfloat16)
    hidden_rounded_state = hidden_act.astype(jnp.bfloat16)
    act_all, tangent_full_rows = (
        lax.all_gather(hidden_rounded_state, "mp", axis=1, tiled=True),
        lax.all_gather(hidden_tangent, "mp", axis=2, tiled=True),
    )
    decoder_full_rows = lax.all_gather(decoder_weight, "dp", axis=0, tiled=True)
    outputs_net = jnp.einsum(
        "sk,ok->so", act_all, decoder_full_rows, preferred_element_type=jnp.float32
    )
    jacobian_predicted = jnp.einsum(
        "mvn,an->mav", tangent_full_rows, decoder_full_rows, preferred_element_type=jnp.float32
    )
    output_residual = (outputs_net - target_mine.astype(jnp.float32)).astype(jnp.bfloat16)
    jacobian_residual = (jacobian_predicted - jac_mine.astype(jnp.float32)).astype(jnp.bfloat16)
    decoder_grad = lax.psum_scatter(
        jnp.einsum("qi,qm->im", output_residual, act_all, preferred_element_type=jnp.float32)
        + jnp.einsum(
            "hzy,hym->zm", jacobian_residual, tangent_full_rows, preferred_element_type=jnp.float32
        ),
        "dp",
        scatter_dimension=0,
        tiled=True,
    )
    act_partial = jnp.einsum(
        "so,oh->sh", output_residual, decoder_full_rows, preferred_element_type=jnp.float32
    )
    tan_partial = jnp.einsum(
        "lud,uf->ldf", jacobian_residual, decoder_full_rows, preferred_element_type=jnp.float32
    )
    act_back, tan_back = (
        lax.psum_scatter(
            act_partial.astype(jnp.bfloat16), "mp", scatter_dimension=1, tiled=True
        ).astype(jnp.float32),
        lax.psum_scatter(
            tan_partial.astype(jnp.bfloat16), "mp", scatter_dimension=2, tiled=True
        ).astype(jnp.float32),
    )
    lin_back = tan_back * hidden_slope[:, None, :]
    pre_back = act_back * hidden_slope - 2.0 * hidden_act * hidden_slope * jnp.sum(
        tan_back * hidden_lin, axis=1
    )
    lin_round = lin_back.astype(jnp.bfloat16)
    pre_round = pre_back.astype(jnp.bfloat16)
    hidden_grad = jnp.einsum(
        "sh,sk->hk", first_round, pre_round, preferred_element_type=jnp.float32
    ) + jnp.einsum("srh,srk->hk", first_tan, lin_round, preferred_element_type=jnp.float32)
    hidden_bgrad = jnp.sum(pre_back, axis=0)
    tan_lower = jnp.einsum(
        "srk,hk->srh", lin_round, hidden_weight, preferred_element_type=jnp.float32
    )
    act_lower = jnp.einsum(
        "sk,hk->sh", pre_round, hidden_weight, preferred_element_type=jnp.float32
    )
    pre_lower = act_lower * first_slope - 2.0 * first_act * first_slope * jnp.sum(
        tan_lower * weight_one[None], axis=1
    )
    weight_part = jnp.einsum(
        "sr,sh->rh", inputs.astype(jnp.float32), pre_lower, precision=lax.Precision.HIGHEST
    ) + jnp.sum(tan_lower * first_slope[:, None, :], axis=0)
    bias_part = jnp.sum(pre_lower, axis=0)
    weight_mid, bias_mid = (
        lax.psum(weight_part.astype(jnp.bfloat16), "mp").astype(jnp.float32),
        lax.psum(bias_part.astype(jnp.bfloat16), "mp").astype(jnp.float32),
    )
    first_weights, first_biases, hidden_weights, hidden_biases = lax.psum(
        (weight_mid, bias_mid, hidden_grad, hidden_bgrad), "dp"
    )
    return (first_weights, first_biases, hidden_weights, hidden_biases, decoder_grad)


def solution(mesh):
    placed = (
        P(),
        P(),
        P(None, ("dp", "mp")),
        P(None, ("dp", "mp"), None),
        P(),
        P(),
        P(None, "mp"),
        P("mp"),
        P(("dp", "mp"), None),
    )
    return jax.shard_map(
        on_device,
        mesh=mesh,
        in_specs=placed,
        out_specs=(P(), P(), P(None, "mp"), P("mp"), P(("dp", "mp"), None)),
        check_vma=False,
    )
```

profile of v0, /device:TPU:0, one launch (start us, length us, event | category | flops | bytes accessed | tf_op | source)
XLA Modules:
  0.0 348.1 jit_solution(14651161969415206212)
XLA Ops:
  7.2 0.0 all-gather.5.cloned.1.call-start
  7.2 0.7 all-gather.5.cloned.1.call-update
  7.9 0.7 compare_select_fusion
  8.6 1.5 gather_fusion
  10.1 0.6 copy.16
  10.7 7.4 %all-to-all-start = ((bf16[16,1,128]{2,1,0:T(2,128)(2,1)}), bf16[16,1,128]{2,1,0:T(2,128)(2,1)S(1)}, u32[]{:S(2)}, u32[]{:S(2)}) async-start(bf16[16,1,128]{2,1,0:T(2,128)(2,1)} %copy.16), calls=%async_computation | async-start | bytes 16384 | tf_op jit(solution)/shard_map/all_to_all | solution.py:23
  18.1 1.2 dynamic_slice.3
  21.3 1.1 fusion.18
  22.4 7.2 %gather_fusion.1 = bf16[16,128,128]{2,1,0:T(8,128)(2,1)} fusion(bf16[512,128,128]{2,1,0:T(8,128)(2,1)} %param.12, s32[1024]{0:T(1024)S(1)} %pad_clamp_fusion), kind=kCustom, calls=%fused_computation.1 | custom fusion | bytes 1048640 | tf_op jit(solution)/shard_map/gather | solution.py:19
  29.6 6.0 %all-to-all-start.1 = ((bf16[16,128,128]{2,1,0:T(8,128)(2,1)}), bf16[16,128,128]{2,1,0:T(8,128)(2,1)S(1)}, u32[]{:S(2)}, u32[]{:S(2)}) async-start(bf16[16,128,128]{2,1,0:T(8,128)(2,1)} %gather_fusion.1), calls=%async_computation.1 | async-start | bytes 1048576 | tf_op jit(solution)/shard_map/all_to_all | solution.py:22
  35.6 0.0 reduce-scatter.10.cloned.1.call-start
  35.7 0.7 fusion.22
  36.4 0.2 fusion.25
  36.6 0.7 fusion.20
  37.3 4.4 %all-gather.2 = bf16[2,1,512]{2,1,0:T(2,128)(2,1)S(1)} all-gather(bf16[1,1,512]{2,1,0:T(2,128)(2,1)S(1)} %reshape.173), channel_id=2, replica_groups=mesh['dp'=16,'mp'=2] {'mp'}, dimensions={0}, use_global_device_ids=true | all-gather | bytes 3072 | tf_op jit(solution)/shard_map/all_gather | solution.py:46
  41.7 2.0 multiply_convert_fusion
  43.7 5.6 %all-gather.1 = bf16[128,1024]{1,0:T(8,128)(2,1)S(1)} all-gather(bf16[128,512]{1,0:T(8,128)(2,1)S(1)} %get-tuple-element.30), channel_id=3, replica_groups=mesh['dp'=16,'mp'=2] {'mp'}, dimensions={1}, use_global_device_ids=true | all-gather | bytes 393216 | tf_op jit(solution)/shard_map/all_gather | solution.py:47
  49.3 6.6 %all-to-all-done.1 = bf16[16,128,128]{2,1,0:T(8,128)(2,1)S(1)} async-done(((bf16[16,128,128]{2,1,0:T(8,128)(2,1)}), bf16[16,128,128]{2,1,0:T(8,128)(2,1)S(1)}, u32[]{:S(2)}, u32[]{:S(2)}) %all-to-all-start.1) | async-done | bytes 524320 | tf_op jit(solution)/shard_map/all_to_all | solution.py:22
  55.9 0.1 bitcast_convert_fusion
  56.0 0.3 copy.18
  56.4 13.1 %all-gather.5.cloned.1.call-done = bf16[2048,1024]{1,0:T(8,128)(2,1)} async-done(((bf16[128,1024]{1,0:T(8,128)(2,1)}), bf16[2048,1024]{1,0:T(8,128)(2,1)}) %all-gather.5.cloned.1.call-update) | async-done | bytes 4194320 | tf_op jit(solution)/shard_map/all_gather | solution.py:49
  69.4 3.5 %fusion.26 = f32[1,2048]{1,0:T(1,128)S(1)} fusion(bf16[1024,1]{0,1:T(2,128)(2,1)S(1)} %bitcast.62, bf16[2048,1024]{1,0:T(8,128)(2,1)} %all-gather.5.cloned.1.call-done), kind=kOutput, calls=%fused_computation.48 | convolution fusion | flops 4194304 | bytes 4204544 | tf_op jit(solution)/shard_map/sk,ok->so/dot_general | solution.py:50
  73.0 0.7 fusion.27
  73.6 0.9 reshape_bitcast_fusion
  74.6 0.0 reduce-scatter.6.cloned.1.call-start
  74.6 3.8 %fusion.1 = bf16[2048,128]{0,1:T(8,128)(2,1)S(1)} fusion(f32[2048,128]{0,1:T(8,128)S(1)} %copy.18, bf16[128,1024]{1,0:T(8,128)(2,1)S(1)} %all-gather.1, bf16[2048,1024]{1,0:T(8,128)(2,1)} %all-gather.5.cloned.1.call-done), kind=kOutput, calls=%fused_computation.5 | convolution fusion | flops 537395200 | bytes 6029312 | tf_op jit(solution)/shard_map/mvn,an->mav/dot_general | solution.py:53
  78.6 1.4 fusion.2
  80.0 0.0 reduce-scatter.6.cloned.1.call-update
  80.0 0.0 all-reduce.5.cloned.1.call-start
  80.1 0.7 bitcast_convert_fusion.1
  80.8 4.4 %reduce-scatter.10.cloned.1.call-done = bf16[512,1]{1,0:T(8,128)(2,1)} async-done(((bf16[1024,1]{1,0:T(8,128)(2,1)}), bf16[512,1]{1,0:T(8,128)(2,1)}) %reduce-scatter.10.cloned.1.call-update) | async-done | bytes 1040
  85.2 1.0 copy.20
  86.2 13.6 %reduce-scatter.6.cloned.1.call-done = bf16[1,128,512]{2,1,0:T(8,128)(2,1)} async-done(((bf16[1,128,1024]{2,1,0:T(8,128)(2,1)}), bf16[1,128,512]{2,1,0:T(8,128)(2,1)}) %reduce-scatter.6.cloned.1.call-update) | async-done | bytes 131088 | tf_op jit(solution)/shard_map/reduce_scatter | solution.py:77
  99.9 1.0 fusion.5
  100.9 0.4 fusion.14
  101.3 1.4 fusion.4
  102.7 0.8 add_convert_fusion
  103.6 0.0 all-reduce.5.cloned.1.call-update
  103.6 0.0 all-reduce.7.cloned.1.call-start
  103.7 1.8 multiply_add_fusion.1
  105.5 0.0 reduce-scatter.8.cloned.1.call-start
  105.6 4.5 %multiply_add_fusion = f32[2048,1024]{1,0:T(8,128)} fusion(bf16[2048,128]{0,1:T(8,128)(2,1)S(1)} %fusion.1, bf16[128,1024]{1,0:T(8,128)(2,1)S(1)} %all-gather.1, f32[1024]{0:T(1024)S(1)} %convert.21, f32[2048]{0:T(1024)S(1)} %get-tuple-element.19), kind=kOutput, calls=%fused_computation.2 | convolution fusion | flops 541065216 | bytes 9187328 | tf_op jit(solution)/shard_map/hzy,hym->zm/dot_general | solution.py:60
  110.1 4.9 %psum.44 = bf16[1024]{0:T(1024)(128)(2,1)S(1)} all-reduce(bf16[1024]{0:T(1024)(128)(2,1)S(1)} %get-tuple-element.25), channel_id=1, replica_groups=mesh['dp'=16,'mp'=2] {'mp'}, use_global_device_ids=true, to_apply=%region_6.0 | all-reduce | flops 1024 | bytes 4096 | tf_op jit(solution)/shard_map/psum | solution.py:106
  115.1 12.0 %all-reduce.5.cloned.1.call-done = bf16[128,1024]{1,0:T(8,128)(2,1)} async-done(((bf16[128,1024]{1,0:T(8,128)(2,1)}), bf16[128,1024]{1,0:T(8,128)(2,1)}) %all-reduce.5.cloned.1.call-update) | async-done | bytes 262160 | tf_op jit(solution)/shard_map/psum | solution.py:105
  127.1 70.9 %all-reduce.8 = (f32[128,1024]{1,0:T(8,128)}, f32[1024]{0:T(1024)}, f32[512]{0:T(512)}) all-reduce(bf16[128,1024]{1,0:T(8,128)(2,1)} %all-reduce.5.cloned.1.call-done, bf16[1024]{0:T(1024)(128)(2,1)S(1)} %psum.44, f32[512]{0:T(512)S(1)} %bitcast.67), channel_id=1, replica_groups=mesh['dp'=16,'mp'=2] {'dp'}, use_global_device_ids=true, to_apply=%region_5.0 | all-reduce | flops 132608 | bytes 796672 | tf_op jit(solution)/shard_map/psum | solution.py:108
  198.0 33.0 %all-reduce.7.cloned.1.call-done = f32[1024,512]{1,0:T(8,128)} async-done(((f32[1024,512]{1,0:T(8,128)}), f32[1024,512]{1,0:T(8,128)}) %all-reduce.7.cloned.1.call-update) | async-done | bytes 2097168 | tf_op jit(solution)/shard_map/psum | solution.py:108
  231.0 107.3 %reduce-scatter.8.cloned.1.call-done = f32[128,1024]{1,0:T(8,128)} async-done(((f32[2048,1024]{1,0:T(8,128)}), f32[128,1024]{1,0:T(8,128)}) %reduce-scatter.8.cloned.1.call-update) | async-done | bytes 524304 | tf_op jit(solution)/shard_map/reduce_scatter | solution.py:58
  338.2 3.1 copy.29
  (34 shorter events, 0.2 us)
Async XLA Ops:
  7.2 29.2 %copy-start = (bf16[1024,512]{1,0:T(8,128)(2,1)S(1)}, bf16[1024,512]{1,0:T(8,128)(2,1)}, u32[]{:S(2)}) copy-start(bf16[1024,512]{1,0:T(8,128)(2,1)} %param.15) | copy-start | bytes 3145732
  7.2 62.2 %all-gather.5.cloned.1.call-start = ((), (), s32[]{:S(2)}) async-start(), calls=%async_computation.5 | async-start | bytes 4456448 | tf_op jit(solution)/shard_map/all_gather | solution.py:49
  10.7 18.9 %all-to-all-start = ((bf16[16,1,128]{2,1,0:T(2,128)(2,1)}), bf16[16,1,128]{2,1,0:T(2,128)(2,1)S(1)}, u32[]{:S(2)}, u32[]{:S(2)}) async-start(bf16[16,1,128]{2,1,0:T(2,128)(2,1)} %copy.16), calls=%async_computation | async-start | bytes 16384 | tf_op jit(solution)/shard_map/all_to_all | solution.py:23
  29.6 26.3 %all-to-all-start.1 = ((bf16[16,128,128]{2,1,0:T(8,128)(2,1)}), bf16[16,128,128]{2,1,0:T(8,128)(2,1)S(1)}, u32[]{:S(2)}, u32[]{:S(2)}) async-start(bf16[16,128,128]{2,1,0:T(8,128)(2,1)} %gather_fusion.1), calls=%async_computation.1 | async-start | bytes 1048576 | tf_op jit(solution)/shard_map/all_to_all | solution.py:22
  35.6 49.6 %reduce-scatter.10.cloned.1.call-start = ((), (), s32[]{:S(2)}) async-start(), calls=%async_computation.10 | async-start | bytes 393216
  69.4 3.6 %copy-start.1 = (bf16[2048,1024]{1,0:T(8,128)(2,1)S(1)}, bf16[2048,1024]{1,0:T(8,128)(2,1)}, u32[]{:S(2)}) copy-start(bf16[2048,1024]{1,0:T(8,128)(2,1)} %all-gather.5.cloned.1.call-done) | copy-start | bytes 12582916
  74.6 25.3 %reduce-scatter.6.cloned.1.call-start = ((), (), s32[]{:S(2)}) async-start(), calls=%async_computation.6 | async-start | bytes 393216 | tf_op jit(solution)/shard_map/reduce_scatter | solution.py:77
  74.6 3.9 %copy-start.2 = (bf16[2048,1024]{1,0:T(8,128)(2,1)S(1)}, bf16[2048,1024]{1,0:T(8,128)(2,1)}, u32[]{:S(2)}) copy-start(bf16[2048,1024]{1,0:T(8,128)(2,1)} %all-gather.5.cloned.1.call-done) | copy-start | bytes 12582916
  78.5 21.4 %copy-start.5 = (f32[128,512]{1,0:T(8,128)S(1)}, f32[128,512]{1,0:T(8,128)}, u32[]{:S(2)}) copy-start(f32[128,512]{1,0:T(8,128)} %get-tuple-element.31) | copy-start | bytes 786436
  78.5 22.4 %copy-start.7 = (bf16[512]{0:T(512)(128)(2,1)S(1)}, bf16[512]{0:T(512)(128)(2,1)}, u32[]{:S(2)}) copy-start(bf16[512]{0:T(512)(128)(2,1)} %param.16) | copy-start | bytes 3076
  78.5 22.8 %copy-start.3 = (bf16[128,1024]{1,0:T(8,128)(2,1)S(1)}, bf16[128,1024]{1,0:T(8,128)(2,1)}, u32[]{:S(2)}) copy-start(bf16[128,1024]{1,0:T(8,128)(2,1)} %param.13) | copy-start | bytes 786436
  78.5 24.2 %copy-start.6 = (bf16[1024]{0:T(1024)(128)(2,1)S(1)}, bf16[1024]{0:T(1024)(128)(2,1)}, u32[]{:S(2)}) copy-start(bf16[1024]{0:T(1024)(128)(2,1)} %param.14) | copy-start | bytes 6148
  80.0 47.1 %all-reduce.5.cloned.1.call-start = ((), (), s32[]{:S(2)}) async-start(), calls=%async_computation.7 | async-start | bytes 524288 | tf_op jit(solution)/shard_map/psum | solution.py:105
  99.9 3.8 %copy-start.4 = (bf16[1,128,512]{2,1,0:T(8,128)(2,1)S(1)}, bf16[1,128,512]{2,1,0:T(8,128)(2,1)}, u32[]{:S(2)}) copy-start(bf16[1,128,512]{2,1,0:T(8,128)(2,1)} %reduce-scatter.6.cloned.1.call-done) | copy-start | bytes 393220
  103.6 127.4 %all-reduce.7.cloned.1.call-start = ((), (), s32[]{:S(2)}) async-start(), calls=%async_computation.8 | async-start | bytes 4194304 | tf_op jit(solution)/shard_map/psum | solution.py:108
  105.5 232.7 %reduce-scatter.8.cloned.1.call-start = ((), (), s32[]{:S(2)}) async-start(), calls=%async_computation.9 | async-start | bytes 8912896 | tf_op jit(solution)/shard_map/reduce_scatter | solution.py:58
Sparse Core Ops, SparseCore 0:
  10.1 59.2 all-gather.4
  74.7 10.4 reduce-scatter.9
  88.0 11.7 reduce-scatter.5
  103.7 23.3 all-reduce.4
  131.1 99.8 all-reduce.6
  235.4 102.7 reduce-scatter.7
where the time goes:
time: 349 us; the launch traced here: 348 us
  waiting for transfers between devices  191 us (55%)
  blocking collectives  85.8 us (25%)
  matrix products  20.9 us (6%)
  between operations  16.3 us (5%)
  local copies, waits for them, and re-layouts  16 us (5%)
  starting transfers between devices  13.6 us (4%)
  other arithmetic  4.8 us (1%)
    reduce_scatter x1, waiting for transfers between devices, on_device(): lax.psum_scatter(jnp.einsum('qi,qm->im', output_residual, act_all, prefer...  107 us
    psum x1, blocking collectives, on_device(): lax.psum((weight_mid, bias_mid, hidden_grad, hidden_bgrad), 'dp')  70.9 us
    psum x1, waiting for transfers between devices, on_device(): lax.psum((weight_mid, bias_mid, hidden_grad, hidden_bgrad), 'dp')  33 us
    reduce_scatter x1, waiting for transfers between devices, on_device(): lax.psum_scatter(tan_partial.astype(jnp.bfloat16), 'mp', scatter_dimensio...  13.6 us
    all_gather x1, waiting for transfers between devices, on_device(): decoder_full_rows = lax.all_gather(decoder_weight, 'dp', axis=0, tiled=True)  13.1 us
    psum x1, waiting for transfers between devices, on_device(): lax.psum(weight_part.astype(jnp.bfloat16), 'mp').astype(jnp.float32)  12 us
    all_to_all x1, starting transfers between devices, on_device(): lax.all_to_all(target_window, 'dp', split_axis=0, concat_axis=1, tiled=True)  7.39 us
    gather x1, local copies, waits for them, and re-layouts, on_device(): jac_window = jac_store[window]  7.22 us
  transfers between devices with their start and end apart: 8, of which 7 were waited for; matrix products, arithmetic and copies ran while one was open for 9% of the time, Pallas kernels for 0%

commit v1 on v0

--- a/solution.py
+++ b/solution.py
@@ -102,7 +102,7 @@
     ) + jnp.sum(tan_lower * first_slope[:, None, :], axis=0)
     bias_part = jnp.sum(pre_lower, axis=0)
     weight_mid, bias_mid = (
-        lax.psum(weight_part.astype(jnp.bfloat16), "mp").astype(jnp.float32),
+        jnp.sum(lax.all_gather(weight_part.astype(jnp.bfloat16), "mp"), axis=0).astype(jnp.float32),
         lax.psum(bias_part.astype(jnp.bfloat16), "mp").astype(jnp.float32),
     )
     first_weights, first_biases, hidden_weights, hidden_biases = lax.psum(

time: 349 us -> 321 us (0.920)
  waiting for transfers between devices: 191 us -> 160 us
  blocking collectives: 85.8 us -> 89.6 us
    psum x1, waiting for transfers between devices: 33 us -> 13.8 us  [on_device(): lax.psum((weight_mid, bias_mid, hidden_grad, hidden_bgrad), 'dp')]
    psum x1 -> x0, waiting for transfers between devices: 12 us -> none  [on_device(): lax.psum(weight_part.astype(jnp.bfloat16), 'mp').astype(jnp.float32)]
    all_gather x0 -> x1, blocking collectives: none -> 7.66 us  [on_device(): lax.all_gather(weight_part.astype(jnp.bfloat16), 'mp')]
    psum x1, blocking collectives: 70.9 us -> 67 us  [on_device(): lax.psum((weight_mid, bias_mid, hidden_grad, hidden_bgrad), 'dp')]
  transfers between devices with their start and end apart: 8 -> 7, of which waited for: 7 -> 6; matrix products, arithmetic and copies ran while one was open for 9% -> 9% of each run, Pallas kernels for 0% -> 0%
where the time goes in v1:
time: 321 us
  waiting for transfers between devices  160 us (50%)
  blocking collectives  89.6 us (28%)
  matrix products  20.9 us (7%)
  local copies, waits for them, and re-layouts  16 us (5%)
  between operations  15.9 us (5%)
  starting transfers between devices  13.6 us (4%)
  other arithmetic  4.18 us (1%)
    reduce_scatter x1, waiting for transfers between devices, on_device(): lax.psum_scatter(jnp.einsum('qi,qm->im', output_residual, act_all, prefer...  107 us
    psum x1, blocking collectives, on_device(): lax.psum((weight_mid, bias_mid, hidden_grad, hidden_bgrad), 'dp')  67 us
    psum x1, waiting for transfers between devices, on_device(): lax.psum((weight_mid, bias_mid, hidden_grad, hidden_bgrad), 'dp')  13.8 us
    reduce_scatter x1, waiting for transfers between devices, on_device(): lax.psum_scatter(tan_partial.astype(jnp.bfloat16), 'mp', scatter_dimensio...  13.6 us
    all_gather x1, waiting for transfers between devices, on_device(): decoder_full_rows = lax.all_gather(decoder_weight, 'dp', axis=0, tiled=True)  13.1 us
    all_gather x1, blocking collectives, on_device(): lax.all_gather(weight_part.astype(jnp.bfloat16), 'mp')  7.66 us
    all_to_all x1, starting transfers between devices, on_device(): lax.all_to_all(target_window, 'dp', split_axis=0, concat_axis=1, tiled=True)  7.39 us
    gather x1, local copies, waits for them, and re-layouts, on_device(): jac_window = jac_store[window]  7.22 us
  transfers between devices with their start and end apart: 7, of which 6 were waited for; matrix products, arithmetic and copies ran while one was open for 9% of the time, Pallas kernels for 0%

profile of v1, /device:TPU:0, one launch (start us, length us, event | category | flops | bytes accessed | tf_op | source)
XLA Modules:
  0.0 320.5 jit_solution(7931420647954568272)
XLA Ops:
  7.2 0.0 all-gather.6.cloned.1.call-start
  7.2 0.7 all-gather.6.cloned.1.call-update
  7.9 0.7 compare_select_fusion
  8.6 1.5 gather_fusion
  10.1 0.6 copy.16
  10.7 7.4 %all-to-all-start = ((bf16[16,1,128]{2,1,0:T(2,128)(2,1)}), bf16[16,1,128]{2,1,0:T(2,128)(2,1)S(1)}, u32[]{:S(2)}, u32[]{:S(2)}) async-start(bf16[16,1,128]{2,1,0:T(2,128)(2,1)} %copy.16), calls=%async_computation | async-start | bytes 16384 | tf_op jit(solution)/shard_map/all_to_all | solution.py:23
  18.1 1.2 dynamic_slice.3
  21.3 1.1 fusion.18
  22.4 7.2 %gather_fusion.1 = bf16[16,128,128]{2,1,0:T(8,128)(2,1)} fusion(bf16[512,128,128]{2,1,0:T(8,128)(2,1)} %param.12, s32[1024]{0:T(1024)S(1)} %pad_clamp_fusion), kind=kCustom, calls=%fused_computation.1 | custom fusion | bytes 1048640 | tf_op jit(solution)/shard_map/gather | solution.py:19
  29.6 6.0 %all-to-all-start.1 = ((bf16[16,128,128]{2,1,0:T(8,128)(2,1)}), bf16[16,128,128]{2,1,0:T(8,128)(2,1)S(1)}, u32[]{:S(2)}, u32[]{:S(2)}) async-start(bf16[16,128,128]{2,1,0:T(8,128)(2,1)} %gather_fusion.1), calls=%async_computation.1 | async-start | bytes 1048576 | tf_op jit(solution)/shard_map/all_to_all | solution.py:22
  35.6 0.0 reduce-scatter.10.cloned.1.call-start
  35.7 0.7 fusion.22
  36.4 0.2 fusion.25
  36.6 0.7 fusion.20
  37.3 4.4 %all-gather.3 = bf16[2,1,512]{2,1,0:T(2,128)(2,1)S(1)} all-gather(bf16[1,1,512]{2,1,0:T(2,128)(2,1)S(1)} %reshape.174), channel_id=2, replica_groups=mesh['dp'=16,'mp'=2] {'mp'}, dimensions={0}, use_global_device_ids=true | all-gather | bytes 3072 | tf_op jit(solution)/shard_map/all_gather | solution.py:46
  41.7 2.0 multiply_convert_fusion
  43.7 5.6 %all-gather.1 = bf16[128,1024]{1,0:T(8,128)(2,1)S(1)} all-gather(bf16[128,512]{1,0:T(8,128)(2,1)S(1)} %get-tuple-element.30), channel_id=3, replica_groups=mesh['dp'=16,'mp'=2] {'mp'}, dimensions={1}, use_global_device_ids=true | all-gather | bytes 393216 | tf_op jit(solution)/shard_map/all_gather | solution.py:47
  49.3 6.6 %all-to-all-done.1 = bf16[16,128,128]{2,1,0:T(8,128)(2,1)S(1)} async-done(((bf16[16,128,128]{2,1,0:T(8,128)(2,1)}), bf16[16,128,128]{2,1,0:T(8,128)(2,1)S(1)}, u32[]{:S(2)}, u32[]{:S(2)}) %all-to-all-start.1) | async-done | bytes 524320 | tf_op jit(solution)/shard_map/all_to_all | solution.py:22
  55.9 0.1 bitcast_convert_fusion
  56.0 0.3 copy.18
  56.4 13.1 %all-gather.6.cloned.1.call-done = bf16[2048,1024]{1,0:T(8,128)(2,1)} async-done(((bf16[128,1024]{1,0:T(8,128)(2,1)}), bf16[2048,1024]{1,0:T(8,128)(2,1)}) %all-gather.6.cloned.1.call-update) | async-done | bytes 4194320 | tf_op jit(solution)/shard_map/all_gather | solution.py:49
  69.4 3.5 %fusion.26 = f32[1,2048]{1,0:T(1,128)S(1)} fusion(bf16[1024,1]{0,1:T(2,128)(2,1)S(1)} %bitcast.66, bf16[2048,1024]{1,0:T(8,128)(2,1)} %all-gather.6.cloned.1.call-done), kind=kOutput, calls=%fused_computation.48 | convolution fusion | flops 4194304 | bytes 4204544 | tf_op jit(solution)/shard_map/sk,ok->so/dot_general | solution.py:50
  73.0 0.7 fusion.27
  73.6 0.9 reshape_bitcast_fusion
  74.6 0.0 reduce-scatter.6.cloned.1.call-start
  74.6 3.8 %fusion.1 = bf16[2048,128]{0,1:T(8,128)(2,1)S(1)} fusion(f32[2048,128]{0,1:T(8,128)S(1)} %copy.18, bf16[128,1024]{1,0:T(8,128)(2,1)S(1)} %all-gather.1, bf16[2048,1024]{1,0:T(8,128)(2,1)} %all-gather.6.cloned.1.call-done), kind=kOutput, calls=%fused_computation.5 | convolution fusion | flops 537395200 | bytes 6029312 | tf_op jit(solution)/shard_map/mvn,an->mav/dot_general | solution.py:53
  78.5 1.4 fusion.2
  80.0 0.0 reduce-scatter.6.cloned.1.call-update
  80.0 0.0 all-reduce.4.cloned.1.call-start
  80.1 5.2 %reduce-scatter.10.cloned.1.call-done = bf16[512,1]{1,0:T(8,128)(2,1)} async-done(((bf16[1024,1]{1,0:T(8,128)(2,1)}), bf16[512,1]{1,0:T(8,128)(2,1)}) %reduce-scatter.10.cloned.1.call-update) | async-done | bytes 1040
  85.2 1.0 copy.20
  86.2 13.6 %reduce-scatter.6.cloned.1.call-done = bf16[1,128,512]{2,1,0:T(8,128)(2,1)} async-done(((bf16[1,128,1024]{2,1,0:T(8,128)(2,1)}), bf16[1,128,512]{2,1,0:T(8,128)(2,1)}) %reduce-scatter.6.cloned.1.call-update) | async-done | bytes 131088 | tf_op jit(solution)/shard_map/reduce_scatter | solution.py:77
  99.9 1.0 fusion.5
  100.9 2.7 multiply_add_fusion.1
  103.6 0.0 all-reduce.4.cloned.1.call-update
  103.6 0.0 reduce-scatter.8.cloned.1.call-start
  103.7 4.5 %multiply_add_fusion = f32[2048,1024]{1,0:T(8,128)} fusion(bf16[2048,128]{0,1:T(8,128)(2,1)S(1)} %fusion.1, bf16[128,1024]{1,0:T(8,128)(2,1)S(1)} %all-gather.1, f32[1024]{0:T(1024)S(1)} %convert.22, f32[2048]{0:T(1024)S(1)} %get-tuple-element.19), kind=kOutput, calls=%fused_computation.2 | convolution fusion | flops 541065216 | bytes 9187328 | tf_op jit(solution)/shard_map/hzy,hym->zm/dot_general | solution.py:60
  108.3 0.7 bitcast_convert_fusion.1
  109.0 0.4 fusion.14
  109.4 0.5 fusion.4
  109.9 4.9 %psum.36 = bf16[1024]{0:T(1024)(128)(2,1)S(1)} all-reduce(bf16[1024]{0:T(1024)(128)(2,1)S(1)} %get-tuple-element.25), channel_id=1, replica_groups=mesh['dp'=16,'mp'=2] {'mp'}, use_global_device_ids=true, to_apply=%region_6.0 | all-reduce | flops 1024 | bytes 4096 | tf_op jit(solution)/shard_map/psum | solution.py:106
  114.8 0.1 add_convert_fusion
  115.0 7.7 %all-gather.2 = bf16[256,1024]{1,0:T(8,128)(2,1)S(1)} all-gather(bf16[128,1024]{1,0:T(8,128)(2,1)S(1)} %add_convert_fusion), channel_id=4, replica_groups=mesh['dp'=16,'mp'=2] {'mp'}, dimensions={0}, use_global_device_ids=true | all-gather | bytes 786432 | tf_op jit(solution)/shard_map/all_gather | solution.py:105
  122.6 0.1 reduce_sum.37
  122.7 67.0 %all-reduce.5 = (f32[128,1024]{1,0:T(8,128)}, f32[1024]{0:T(1024)}, f32[512]{0:T(512)}) all-reduce(bf16[128,1024]{1,0:T(8,128)(2,1)S(1)} %reduce_sum.37, bf16[1024]{0:T(1024)(128)(2,1)S(1)} %psum.36, f32[512]{0:T(512)S(1)} %bitcast.69), channel_id=1, replica_groups=mesh['dp'=16,'mp'=2] {'dp'}, use_global_device_ids=true, to_apply=%region_5.0 | all-reduce | flops 132608 | bytes 796672 | tf_op jit(solution)/shard_map/psum | solution.py:108
  189.7 13.8 %all-reduce.4.cloned.1.call-done = f32[1024,512]{1,0:T(8,128)} async-done(((f32[1024,512]{1,0:T(8,128)}), f32[1024,512]{1,0:T(8,128)}) %all-reduce.4.cloned.1.call-update) | async-done | bytes 2097168 | tf_op jit(solution)/shard_map/psum | solution.py:108
  203.6 107.3 %reduce-scatter.8.cloned.1.call-done = f32[128,1024]{1,0:T(8,128)} async-done(((f32[2048,1024]{1,0:T(8,128)}), f32[128,1024]{1,0:T(8,128)}) %reduce-scatter.8.cloned.1.call-update) | async-done | bytes 524304 | tf_op jit(solution)/shard_map/reduce_scatter | solution.py:58
  310.9 3.1 copy.28
  (33 shorter events, 0.2 us)
Async XLA Ops:
  7.2 29.2 %copy-start = (bf16[1024,512]{1,0:T(8,128)(2,1)S(1)}, bf16[1024,512]{1,0:T(8,128)(2,1)}, u32[]{:S(2)}) copy-start(bf16[1024,512]{1,0:T(8,128)(2,1)} %param.15) | copy-start | bytes 3145732
  7.2 62.2 %all-gather.6.cloned.1.call-start = ((), (), s32[]{:S(2)}) async-start(), calls=%async_computation.5 | async-start | bytes 4456448 | tf_op jit(solution)/shard_map/all_gather | solution.py:49
  10.7 18.9 %all-to-all-start = ((bf16[16,1,128]{2,1,0:T(2,128)(2,1)}), bf16[16,1,128]{2,1,0:T(2,128)(2,1)S(1)}, u32[]{:S(2)}, u32[]{:S(2)}) async-start(bf16[16,1,128]{2,1,0:T(2,128)(2,1)} %copy.16), calls=%async_computation | async-start | bytes 16384 | tf_op jit(solution)/shard_map/all_to_all | solution.py:23
  29.6 26.3 %all-to-all-start.1 = ((bf16[16,128,128]{2,1,0:T(8,128)(2,1)}), bf16[16,128,128]{2,1,0:T(8,128)(2,1)S(1)}, u32[]{:S(2)}, u32[]{:S(2)}) async-start(bf16[16,128,128]{2,1,0:T(8,128)(2,1)} %gather_fusion.1), calls=%async_computation.1 | async-start | bytes 1048576 | tf_op jit(solution)/shard_map/all_to_all | solution.py:22
  35.6 49.6 %reduce-scatter.10.cloned.1.call-start = ((), (), s32[]{:S(2)}) async-start(), calls=%async_computation.9 | async-start | bytes 393216
  69.4 3.6 %copy-start.1 = (bf16[2048,1024]{1,0:T(8,128)(2,1)S(1)}, bf16[2048,1024]{1,0:T(8,128)(2,1)}, u32[]{:S(2)}) copy-start(bf16[2048,1024]{1,0:T(8,128)(2,1)} %all-gather.6.cloned.1.call-done) | copy-start | bytes 12582916
  74.6 25.3 %reduce-scatter.6.cloned.1.call-start = ((), (), s32[]{:S(2)}) async-start(), calls=%async_computation.6 | async-start | bytes 393216 | tf_op jit(solution)/shard_map/reduce_scatter | solution.py:77
  74.6 3.9 %copy-start.2 = (bf16[2048,1024]{1,0:T(8,128)(2,1)S(1)}, bf16[2048,1024]{1,0:T(8,128)(2,1)}, u32[]{:S(2)}) copy-start(bf16[2048,1024]{1,0:T(8,128)(2,1)} %all-gather.6.cloned.1.call-done) | copy-start | bytes 12582916
  78.5 21.4 %copy-start.5 = (f32[128,512]{1,0:T(8,128)S(1)}, f32[128,512]{1,0:T(8,128)}, u32[]{:S(2)}) copy-start(f32[128,512]{1,0:T(8,128)} %get-tuple-element.31) | copy-start | bytes 786436
  78.5 22.3 %copy-start.7 = (bf16[512]{0:T(512)(128)(2,1)S(1)}, bf16[512]{0:T(512)(128)(2,1)}, u32[]{:S(2)}) copy-start(bf16[512]{0:T(512)(128)(2,1)} %param.16) | copy-start | bytes 3076
  78.5 22.3 %copy-start.3 = (bf16[128,1024]{1,0:T(8,128)(2,1)S(1)}, bf16[128,1024]{1,0:T(8,128)(2,1)}, u32[]{:S(2)}) copy-start(bf16[128,1024]{1,0:T(8,128)(2,1)} %param.13) | copy-start | bytes 786436
  80.0 123.5 %all-reduce.4.cloned.1.call-start = ((), (), s32[]{:S(2)}) async-start(), calls=%async_computation.7 | async-start | bytes 4194304 | tf_op jit(solution)/shard_map/psum | solution.py:108
  103.6 207.3 %reduce-scatter.8.cloned.1.call-start = ((), (), s32[]{:S(2)}) async-start(), calls=%async_computation.8 | async-start | bytes 8912896 | tf_op jit(solution)/shard_map/reduce_scatter | solution.py:58
  108.2 1.1 copy-start.4
  108.2 1.7 copy-start.6
Sparse Core Ops, SparseCore 0:
  10.1 59.2 all-gather.5
  74.7 10.4 reduce-scatter.9
  88.0 11.7 reduce-scatter.5
  103.8 99.6 all-reduce.3
  208.0 102.8 reduce-scatter.7
